TPU v7x, 32 devices: a whole 2x2x4 slice. The times are simulated.
32 devices in a mesh: parts: 2 (over x), frame: 2 (over core), tile: 8 (over z, y).
Axes of the slice: x: 2, y: 2, z: 4, core: 2. Of those that a mesh axis runs over, the one named last changes fastest.
Arguments:
- decoded_refs: bfloat16 [64, 96, 64, 256], P(('parts', 'frame'), None, 'tile'), parts along dimension 0, may hold values from -6 to 6
- current_frames: bfloat16 [16, 96, 64, 256], P(('parts', 'frame'), None, 'tile'), parts along dimension 0, may hold values from -6 to 6
- ref_pairs: int32 [16, 2], P('parts'), parts along dimension 0, may hold values from 0 to 31
- ref_slots: int32 [64], P('parts'), parts along dimension 0, may hold values from 0 to 31, each once
- frame_numbers: int32 [16], P('parts'), parts along dimension 0, may hold values from 0 to 31
- rate_weights: float32 [64], P('parts'), parts along dimension 0, may hold values from 0.5 to 4
- join_kernel: bfloat16 [3, 3, 96, 288], replicated, may hold values from -0.125 to 0.125
- out_kernel: bfloat16 [3, 3, 96, 96], replicated, may hold values from -0.21875 to 0.21875
Outputs:
- reconstruction: bfloat16 [16, 96, 64, 256], P(('parts', 'frame'), None, 'tile'), parts along dimension 0
- join_grad: float32 [6, 3, 96, 288], P('parts'), parts along dimension 0
- output_grad: float32 [6, 3, 96, 96], P('parts'), parts along dimension 0
There are 2 independent parts, one for each index of `parts`. A program takes and returns all parts, laid end to end along the dimension named above; an argument that names none is the same for every part. Nothing has to cross between parts.
Inputs may be any that keep to these rules, and one draw needn't show every extreme that they name: `ref_pairs`: each B-frame names two decoded frames, possibly the same one. `ref_slots`: each slot holds exactly one decoded frame.
All inputs are finite; a program needn't handle non-finite values.
Results may differ from a plain program's by a relative error of at most 0.005.
Values may be sent and summed in bfloat16 or wider, within the bound.
No kernel may reach another device: no remote copies, remote signals or barrier semaphores. Data moves between devices by JAX's collectives and lax.ppermute only.
A program may use at most 128 MiB of HBM per device.

v0:
```python
import jax
import jax.numpy as jnp
from jax import lax
from jax.sharding import PartitionSpec as P


def partner(array, axis, stride):
    return lax.ppermute(array, axis, [(i, i ^ 1 << stride) for i in range(lax.axis_size(axis))])


def with_halo(cells, sides, width):
    for axis, dim in sides:
        count = lax.axis_size(axis)
        ends = count - 1
        head = lax.slice_in_dim(cells, 0, width, axis=dim)
        tail = lax.slice_in_dim(cells, cells.shape[dim] - width, cells.shape[dim], axis=dim)
        cells = jnp.concatenate(
            [
                lax.ppermute(tail, axis, [(i, (i + 1) % count) for i in range(ends)]),
                cells,
                lax.ppermute(head, axis, [((i + 1) % count, i) for i in range(ends)]),
            ],
            axis=dim,
        )
    return cells


def pad_cols(field):
    return jnp.pad(field, ((0, 0), (0, 0), (0, 0), (1, 1)))


def apply_taps(padded, kernel, row_count, col_count):
    running = None
    for row_tap in range(3):
        for col_tap in range(3):
            window = padded[:, :, row_tap : row_tap + row_count, col_tap : col_tap + col_count]
            partial_sum = jnp.einsum(
                "oi,bihw->bohw",
                kernel[row_tap, col_tap],
                window,
                preferred_element_type=jnp.float32,
            )
            running = partial_sum if running is None else running + partial_sum
    return running


def tap_grads(upstream, padded, row_count, col_count):
    pieces = []
    for row_tap in range(3):
        for col_tap in range(3):
            window = padded[:, :, row_tap : row_tap + row_count, col_tap : col_tap + col_count]
            pieces.append(
                jnp.einsum("bohw,bihw->oi", upstream, window, preferred_element_type=jnp.float32)
            )
    stacked = jnp.stack(pieces)
    return stacked.reshape((3, 3) + stacked.shape[1:])


def transpose_taps(padded, kernel, row_count, col_count):
    running = None
    for row_tap in range(3):
        for col_tap in range(3):
            window = padded[
                :, :, 2 - row_tap : 2 - row_tap + row_count, 2 - col_tap : 2 - col_tap + col_count
            ]
            partial_sum = jnp.einsum(
                "oi,bohw->bihw",
                kernel[row_tap, col_tap],
                window,
                preferred_element_type=jnp.float32,
            )
            running = partial_sum if running is None else running + partial_sum
    return running


def on_device(
    decoded_refs,
    current_frames,
    ref_pairs,
    ref_slots,
    frame_numbers,
    rate_weights,
    join_kernel,
    out_kernel,
):
    local_refs = decoded_refs.shape[0]
    local_frames, channels, tile_rows, col_count = current_frames.shape
    group = lax.axis_index("frame")
    frame_range = jnp.arange(ref_slots.shape[0], dtype=jnp.int32)

    def pair_slots(which):
        pairs = lax.dynamic_slice_in_dim(ref_pairs, which * local_frames, local_frames, 0)
        return jnp.sum(jnp.where(pairs[:, :, None] == frame_range, ref_slots, 0), axis=-1).reshape(
            -1
        )

    mine = pair_slots(group)
    other = pair_slots(1 - group) - group * local_refs
    other_held = (other >= 0) & (other < local_refs)
    outgoing = jnp.take(decoded_refs, jnp.clip(other, 0, local_refs - 1), axis=0)
    outgoing = jnp.where(other_held[:, None, None, None], outgoing, jnp.zeros((), jnp.bfloat16))
    incoming = partner(outgoing, "frame", 0)
    mine_local = mine - group * local_refs
    mine_held = (mine_local >= 0) & (mine_local < local_refs)
    own_tiles = jnp.take(decoded_refs, jnp.clip(mine_local, 0, local_refs - 1), axis=0)
    picked = jnp.where(mine_held[:, None, None, None], own_tiles, incoming)
    picked = picked.reshape(local_frames, 2 * channels, tile_rows, col_count)
    stacked = jnp.concatenate([picked, current_frames], axis=1)
    height = tile_rows * lax.axis_size("tile")
    stacked_pad = pad_cols(with_halo(stacked, (("tile", 2),), 1))
    preact = apply_taps(stacked_pad, join_kernel, tile_rows, col_count)
    hidden = jax.nn.silu(preact).astype(jnp.bfloat16)
    hidden_pad = pad_cols(with_halo(hidden, (("tile", 2),), 1))
    recon = apply_taps(hidden_pad, out_kernel, tile_rows, col_count)
    frames_here = lax.dynamic_slice_in_dim(frame_numbers, group * local_frames, local_frames, 0)
    gop_range = jnp.arange(rate_weights.shape[0], dtype=jnp.int32)
    weight_here = jnp.sum(jnp.where(frames_here[:, None] == gop_range, rate_weights, 0.0), axis=-1)
    residual = (
        2.0
        * weight_here[:, None, None, None]
        * (recon - current_frames.astype(jnp.float32))
        / (height * col_count)
    ).astype(jnp.bfloat16)
    output_part = tap_grads(residual, hidden_pad, tile_rows, col_count)
    residual_pad = pad_cols(with_halo(residual, (("tile", 2),), 1))
    hidden_grad = transpose_taps(residual_pad, out_kernel, tile_rows, col_count)
    sigma = jax.nn.sigmoid(preact)
    preact_grad = (hidden_grad * (sigma * (1.0 + preact * (1.0 - sigma)))).astype(jnp.bfloat16)
    join_part = tap_grads(preact_grad, stacked_pad, tile_rows, col_count)
    join_total, output_total = lax.psum((join_part, output_part), ("frame", "tile"))
    return (recon.astype(jnp.bfloat16), join_total, output_total)


def solution(mesh):
    placed = (
        P(("parts", "frame"), None, "tile", None),
        P(("parts", "frame"), None, "tile", None),
        P("parts", None),
        P("parts"),
        P("parts"),
        P("parts"),
        P(),
        P(),
    )
    return jax.shard_map(
        on_device,
        mesh=mesh,
        in_specs=placed,
        out_specs=(
            P(("parts", "frame"), None, "tile", None),
            P("parts", None, None, None),
            P("parts", None, None, None),
        ),
        check_vma=False,
    )
```

profile of v0, /device:TPU:0, one launch (start us, length us, event | category | flops | bytes accessed | tf_op | source)
XLA Modules:
  0.0 316.3 jit_solution(6652373692335212695)
XLA Ops:
  9.5 3.5 %gather_fusion.1 = bf16[8,96,8,256]{3,2,1,0:T(8,128)(2,1)S(1)} fusion(bf16[16,96,8,256]{3,2,1,0:T(8,128)(2,1)} %param.10, s32[1024]{0:T(1024)S(1)} %pad_clamp_fusion), kind=kCustom, calls=%fused_computation.1.clone | custom fusion | bytes 6291488 | tf_op jit(solution)/shard_map/jit(_take)/gather | solution.py:100
  15.9 3.5 %gather_fusion = bf16[8,96,8,256]{3,2,1,0:T(8,128)(2,1)S(1)} fusion(bf16[16,96,8,256]{3,2,1,0:T(8,128)(2,1)} %param.10, s32[1024]{0:T(1024)S(1)} %pad_clamp_fusion.1), kind=kCustom, calls=%fused_computation.clone | custom fusion | bytes 6291488 | tf_op jit(solution)/shard_map/jit(_take)/gather | solution.py:105
  21.3 2.3 select_select_fusion.1
  25.4 4.8 %collective-permute-start.1 = (bf16[4,288,1,256]{3,1,2,0:T(8,128)(2,1)S(1)}, bf16[4,288,1,256]{3,1,2,0:T(8,128)(2,1)S(1)}, u32[]{:S(2)}, u32[]{:S(2)}) collective-permute-start(bf16[4,288,1,256]{3,1,2,0:T(8,128)(2,1)S(1)} %get-tuple-element.17), channel_id=1, source_target_pairs={{0,1},{1,2},{2,3},{3,4},{4,5},{5,6},{6,7},{8,9},{9,10},{10,11},{11... | collective-permute-start | bytes 1769480 | tf_op jit(solution)/shard_map/ppermute | solution.py:19
  31.9 3.0 fusion.184
  34.9 20.8 %collective-permute-done.1 = bf16[4,288,1,256]{3,1,2,0:T(8,128)(2,1)S(1)} collective-permute-done((bf16[4,288,1,256]{3,1,2,0:T(8,128)(2,1)S(1)}, bf16[4,288,1,256]{3,1,2,0:T(8,128)(2,1)S(1)}, u32[]{:S(2)}, u32[]{:S(2)}) %collective-permute-start.1) | collective-permute-done | bytes 589856 | tf_op jit(solution)/shard_map/ppermute | solution.py:19
  55.8 5.9 %fusion.5 = bf16[4,288,10,258]{3,1,2,0:T(8,128)(2,1)S(1)} fusion(bf16[4,288,1,256]{3,1,2,0:T(8,128)(2,1)S(1)} %collective-permute-done.2, bf16[4,288,8,256]{3,1,2,0:T(8,128)(2,1)S(1)} %copy_dynamic-update-slice_fusion.1, bf16[4,288,1,256]{3,1,2,0:T(8,128)(2,1)S(1)} %collective-permute-done.1), kind=kLoop, calls=%fused_computation.9 | loop fusion | flops 35665920 | bytes 11842560 | tf_op jit(solution)/shard_map/concatenate | solution.py:17
  61.7 3.0 fusion.13
  64.7 3.3 %fusion.17 = f32[4,8,256,96]{2,3,1,0:T(8,128)} fusion(bf16[4,288,10,258]{3,1,2,0:T(8,128)(2,1)S(1)} %fusion.5, bf16[3,3,96,288]{3,2,1,0:T(8,128)(2,1)S(1)} %copy-done.8), kind=kOutput, calls=%fused_computation.25 | convolution fusion | flops 452984832 | bytes 7938048 | tf_op jit(solution)/shard_map/oi,bihw->bohw/dot_general | solution.py:37
  68.0 3.0 fusion.21
  71.0 3.3 %fusion.25 = f32[4,8,256,96]{2,3,1,0:T(8,128)} fusion(bf16[4,288,10,258]{3,1,2,0:T(8,128)(2,1)S(1)} %fusion.5, bf16[3,3,96,288]{3,2,1,0:T(8,128)(2,1)S(1)} %copy-done.8), kind=kOutput, calls=%fused_computation.33 | convolution fusion | flops 452984832 | bytes 7938048 | tf_op jit(solution)/shard_map/oi,bihw->bohw/dot_general | solution.py:37
  74.3 3.0 fusion.29
  77.2 3.0 fusion.44
  80.3 3.0 fusion.42
  83.2 11.2 %fusion.38 = (bf16[4,96,8,256]{3,1,2,0:T(8,128)(2,1)}, f32[4,8,256,96]{2,3,1,0:T(8,128)}) fusion(bf16[4,288,10,258]{3,1,2,0:T(8,128)(2,1)S(1)} %fusion.5, bf16[3,3,96,288]{3,2,1,0:T(8,128)(2,1)} %param.16, f32[4,8,256,96]{2,3,1,0:T(8,128)} %fusion.44, f32[4,8,256,96]{2,3,1,0:T(8,128)} %fusion.13, f32[4,8,256,96]{2,3,1,0:T(8,128)} %fusion.17, ...), kind=kOutput, calls=%fused_computation.52 | convolution fusion | flops 463208448 | bytes 34676736 | tf_op jit(solution)/shard_map/oi,bihw->bohw/dot_general | solution.py:37
  95.6 4.4 %collective-permute-start.3 = (bf16[4,96,1,256]{3,1,2,0:T(8,128)(2,1)S(1)}, bf16[4,96,1,256]{3,1,2,0:T(8,128)(2,1)S(1)}, u32[]{:S(2)}, u32[]{:S(2)}) collective-permute-start(bf16[4,96,1,256]{3,1,2,0:T(8,128)(2,1)S(1)} %get-tuple-element.21), channel_id=1, source_target_pairs={{0,1},{1,2},{2,3},{3,4},{4,5},{5,6},{6,7},{8,9},{9,10},{10,11},{11... | collective-permute-start | bytes 589832 | tf_op jit(solution)/shard_map/ppermute | solution.py:19
  101.8 3.7 %fusion.209 = f32[4,8,256,96]{2,3,1,0:T(8,128)} fusion(bf16[4,96,8,256]{3,1,2,0:T(8,128)(2,1)} %get-tuple-element.25, bf16[3,3,96,96]{3,2,1,0:T(8,128)(2,1)S(1)} %copy-done.4), kind=kOutput, calls=%fused_computation.183 | convolution fusion | flops 150994944 | bytes 4743168 | tf_op jit(solution)/shard_map/oi,bihw->bohw/dot_general | solution.py:37
  105.5 3.6 %collective-permute-done.4 = bf16[4,96,1,256]{3,1,2,0:T(8,128)(2,1)S(1)} collective-permute-done((bf16[4,96,1,256]{3,1,2,0:T(8,128)(2,1)S(1)}, bf16[4,96,1,256]{3,1,2,0:T(8,128)(2,1)S(1)}, u32[]{:S(2)}, u32[]{:S(2)}) %collective-permute-start.4) | collective-permute-done | bytes 196640 | tf_op jit(solution)/shard_map/ppermute | solution.py:21
  113.3 2.4 fusion.80
  117.9 2.3 fusion.88
  126.9 12.3 %bitcast_convert_fusion = (bf16[4,96,8,256]{3,1,2,0:T(8,128)(2,1)}, f32[4,8,256,96]{2,3,1,0:T(8,128)}) fusion(bf16[4,96,10,258]{3,1,2,0:T(8,128)(2,1)S(1)} %select_maximum_fusion.2, bf16[3,3,96,96]{3,2,1,0:T(8,128)(2,1)S(1)} %copy-done.4, f32[4,8,256,96]{2,3,1,0:T(8,128)} %fusion.175, f32[4,8,256,96]{2,3,1,0:T(8,128)} %fusion.76, ...), kind=kOutput, calls=%fused_computation.42 | convolution fusion | flops 158072832 | bytes 31481856 | tf_op jit(solution)/shard_map/oi,bihw->bohw/dot_general | solution.py:37
  139.2 2.6 fusion.34
  146.0 5.4 %collective-permute-start.5 = (bf16[4,96,1,256]{3,1,2,0:T(8,128)(2,1)S(1)}, bf16[4,96,1,256]{3,1,2,0:T(8,128)(2,1)S(1)}, u32[]{:S(2)}, u32[]{:S(2)}) collective-permute-start(bf16[4,96,1,256]{3,1,2,0:T(8,128)(2,1)S(1)} %get-tuple-element.20), channel_id=1, source_target_pairs={{0,1},{1,2},{2,3},{3,4},{4,5},{5,6},{6,7},{8,9},{9,10},{10,11},{11... | collective-permute-start | bytes 589832 | tf_op jit(solution)/shard_map/ppermute | solution.py:19
  160.6 2.5 fusion.58
  163.1 2.3 fusion.60
  165.4 2.4 fusion.62
  170.1 2.5 fusion.66
  174.8 2.3 fusion.46
  177.1 10.6 %fusion.31 = bf16[4,96,8,256]{3,1,2,0:T(8,128)(2,1)S(1)} fusion(f32[4,8,256,96]{2,3,1,0:T(8,128)} %get-tuple-element.26, f32[4,8,256,96]{2,3,1,0:T(8,128)} %fusion.50, f32[4,8,256,96]{2,3,1,0:T(8,128)} %fusion.58, f32[4,8,256,96]{2,3,1,0:T(8,128)} %fusion.60, f32[4,8,256,96]{2,3,1,0:T(8,128)} %fusion.207, f32[4,8,256,96]{2,3,1,0:T(8,128)} %fusion.62, ...), kind=kOutput, calls=%fused_computation.40 | convolution fusion | flops 164364288 | bytes 31481856 | tf_op jit(solution)/shard_map/oi,bohw->bihw/dot_general | solution.py:66
  206.3 3.4 %copy.56 = bf16[4,96,8,256]{3,2,1,0:T(8,128)(2,1)} copy(bf16[4,96,8,256]{3,1,2,0:T(8,128)(2,1)} %get-tuple-element.27) | data formatting | bytes 3145728
  209.7 95.2 %all-reduce.6.cloned.1.call-done = (f32[3,3,96,288]{3,2,1,0:T(8,128)}, f32[3,3,96,96]{3,2,1,0:T(8,128)}) async-done(((f32[3,3,96,288]{3,2,1,0:T(8,128)}, f32[3,3,96,96]{3,2,1,0:T(8,128)}), (f32[3,3,96,288]{3,2,1,0:T(8,128)}, f32[3,3,96,96]{3,2,1,0:T(8,128)})) %all-reduce.6.cloned.1.call-update) | async-done | bytes 1327120 | tf_op jit(solution)/shard_map/psum | solution.py:130
  304.9 2.5 copy.133
  (89 shorter events, 64.6 us)
Async XLA Ops:
  7.2 297.8 %all-reduce.6.cloned.1.call-start = ((), (), s32[]{:S(2)}) async-start(), calls=%async_computation | async-start | bytes 3538944 | tf_op jit(solution)/shard_map/psum | solution.py:130
  13.1 2.6 copy-start.9
  15.2 6.1 %collective-permute-start = (bf16[8,96,8,256]{3,2,1,0:T(8,128)(2,1)}, bf16[8,96,8,256]{3,2,1,0:T(8,128)(2,1)}, u32[]{:S(2)}, u32[]{:S(2)}) collective-permute-start(bf16[8,96,8,256]{3,2,1,0:T(8,128)(2,1)} %select_select_fusion), channel_id=1, source_target_pairs={{0,8},{8,0},{1,9},{9,1},{2,10},{10,2},{3,11},{11,3},{4,12},{12,4},... | collective-permute-start | bytes 9437192 | tf_op jit(solution)/shard_map/ppermute | solution.py:8
  15.9 3.6 %copy-start.10 = (f32[32]{0:T(128)S(1)}, f32[32]{0:T(128)}, u32[]{:S(2)}) copy-start(f32[32]{0:T(128)} %param.15) | copy-start | bytes 388
  23.6 1.4 copy-start.1
  25.0 6.9 %copy-start.8 = (bf16[3,3,96,288]{3,2,1,0:T(8,128)(2,1)S(1)}, bf16[3,3,96,288]{3,2,1,0:T(8,128)(2,1)}, u32[]{:S(2)}) copy-start(bf16[3,3,96,288]{3,2,1,0:T(8,128)(2,1)} %param.16) | copy-start | bytes 1492996
  25.4 30.3 %collective-permute-start.1 = (bf16[4,288,1,256]{3,1,2,0:T(8,128)(2,1)S(1)}, bf16[4,288,1,256]{3,1,2,0:T(8,128)(2,1)S(1)}, u32[]{:S(2)}, u32[]{:S(2)}) collective-permute-start(bf16[4,288,1,256]{3,1,2,0:T(8,128)(2,1)S(1)} %get-tuple-element.17), channel_id=1, source_target_pairs={{0,1},{1,2},{2,3},{3,4},{4,5},{5,6},{6,7},{8,9},{9,10},{10,11},{11... | collective-permute-start | bytes 1769480 | tf_op jit(solution)/shard_map/ppermute | solution.py:19
  30.3 25.5 %collective-permute-start.2 = (bf16[4,288,1,256]{3,1,2,0:T(8,128)(2,1)S(1)}, bf16[4,288,1,256]{3,1,2,0:T(8,128)(2,1)S(1)}, u32[]{:S(2)}, u32[]{:S(2)}) collective-permute-start(bf16[4,288,1,256]{3,1,2,0:T(8,128)(2,1)S(1)} %get-tuple-element.18), channel_id=1, source_target_pairs={{1,0},{2,1},{3,2},{4,3},{5,4},{6,5},{7,6},{9,8},{10,9},{11,10},{12... | collective-permute-start | bytes 1769480 | tf_op jit(solution)/shard_map/ppermute | solution.py:21
  55.7 24.5 %copy-start.5 = (bf16[4,288,1,256]{3,1,2,0:T(8,128)(2,1)}, bf16[4,288,1,256]{3,1,2,0:T(8,128)(2,1)S(1)}, u32[]{:S(2)}) copy-start(bf16[4,288,1,256]{3,1,2,0:T(8,128)(2,1)S(1)} %collective-permute-done.1) | copy-start | bytes 1769476
  83.2 18.6 %copy-start.4 = (bf16[3,3,96,96]{3,2,1,0:T(8,128)(2,1)S(1)}, bf16[3,3,96,96]{3,2,1,0:T(8,128)(2,1)}, u32[]{:S(2)}) copy-start(bf16[3,3,96,96]{3,2,1,0:T(8,128)(2,1)} %param.17) | copy-start | bytes 497668
  94.4 14.7 %copy-start = (bf16[4,96,8,256]{3,1,2,0:T(8,128)(2,1)S(1)}, bf16[4,96,8,256]{3,1,2,0:T(8,128)(2,1)}, u32[]{:S(2)}) copy-start(bf16[4,96,8,256]{3,1,2,0:T(8,128)(2,1)} %get-tuple-element.25) | copy-start | bytes 4718596
  95.6 9.9 %collective-permute-start.3 = (bf16[4,96,1,256]{3,1,2,0:T(8,128)(2,1)S(1)}, bf16[4,96,1,256]{3,1,2,0:T(8,128)(2,1)S(1)}, u32[]{:S(2)}, u32[]{:S(2)}) collective-permute-start(bf16[4,96,1,256]{3,1,2,0:T(8,128)(2,1)S(1)} %get-tuple-element.21), channel_id=1, source_target_pairs={{0,1},{1,2},{2,3},{3,4},{4,5},{5,6},{6,7},{8,9},{9,10},{10,11},{11... | collective-permute-start | bytes 589832 | tf_op jit(solution)/shard_map/ppermute | solution.py:19
  100.0 9.1 %collective-permute-start.4 = (bf16[4,96,1,256]{3,1,2,0:T(8,128)(2,1)S(1)}, bf16[4,96,1,256]{3,1,2,0:T(8,128)(2,1)S(1)}, u32[]{:S(2)}, u32[]{:S(2)}) collective-permute-start(bf16[4,96,1,256]{3,1,2,0:T(8,128)(2,1)S(1)} %get-tuple-element.22), channel_id=1, source_target_pairs={{1,0},{2,1},{3,2},{4,3},{5,4},{6,5},{7,6},{9,8},{10,9},{11,10},{12... | collective-permute-start | bytes 589832 | tf_op jit(solution)/shard_map/ppermute | solution.py:21
  126.9 12.3 %copy-start.2 = (bf16[4,96,8,256]{3,2,1,0:T(8,128)(2,1)S(1)}, bf16[4,96,8,256]{3,2,1,0:T(8,128)(2,1)}, u32[]{:S(2)}) copy-start(bf16[4,96,8,256]{3,2,1,0:T(8,128)(2,1)} %param.11) | copy-start | bytes 4718596
  144.8 11.9 %collective-permute-start.6 = (bf16[4,96,1,256]{3,1,2,0:T(8,128)(2,1)S(1)}, bf16[4,96,1,256]{3,1,2,0:T(8,128)(2,1)S(1)}, u32[]{:S(2)}, u32[]{:S(2)}) collective-permute-start(bf16[4,96,1,256]{3,1,2,0:T(8,128)(2,1)S(1)} %get-tuple-element.19), channel_id=1, source_target_pairs={{1,0},{2,1},{3,2},{4,3},{5,4},{6,5},{7,6},{9,8},{10,9},{11,10},{12... | collective-permute-start | bytes 589832 | tf_op jit(solution)/shard_map/ppermute | solution.py:21
  146.0 12.6 %collective-permute-start.5 = (bf16[4,96,1,256]{3,1,2,0:T(8,128)(2,1)S(1)}, bf16[4,96,1,256]{3,1,2,0:T(8,128)(2,1)S(1)}, u32[]{:S(2)}, u32[]{:S(2)}) collective-permute-start(bf16[4,96,1,256]{3,1,2,0:T(8,128)(2,1)S(1)} %get-tuple-element.20), channel_id=1, source_target_pairs={{0,1},{1,2},{2,3},{3,4},{4,5},{5,6},{6,7},{8,9},{9,10},{10,11},{11... | collective-permute-start | bytes 589832 | tf_op jit(solution)/shard_map/ppermute | solution.py:19
  156.6 6.4 %copy-start.7 = (f32[9,96,96]{2,1,0:T(8,128)}, f32[9,96,96]{2,1,0:T(8,128)S(1)}, u32[]{:S(2)}) copy-start(f32[9,96,96]{2,1,0:T(8,128)S(1)} %fusion.168) | copy-start | bytes 995332
  187.7 1.8 copy-start.6
  205.2 1.1 copy-start.3
Sparse Core Ops, SparseCore 0:
  206.4 98.4 all-reduce.5
where the time goes:
time: 320 us; the launch traced here: 316 us
  waiting for transfers between devices  123 us (38%)
  matrix products  120 us (38%)
  local copies, waits for them, and re-layouts  20.6 us (6%)
  starting transfers between devices  19.8 us (6%)
  other arithmetic  18 us (6%)
  between operations  14.7 us (5%)
    psum x1, waiting for transfers between devices, on_device(): lax.psum((join_part, output_part), ('frame', 'tile'))  95.2 us
    dot_general x18, matrix products, apply_taps(): jnp.einsum('oi,bihw->bohw', kernel[row_tap, col_tap], window, preferred_e...  67.6 us
    dot_general x9, matrix products, transpose_taps(): jnp.einsum('oi,bohw->bihw', kernel[row_tap, col_tap], window, preferred_e...  29.4 us
    dot_general x18, matrix products, tap_grads(): jnp.einsum('bohw,bihw->oi', upstream, window, preferred_element_type=jnp....  23.1 us
    ppermute x3, waiting for transfers between devices, with_halo(): lax.ppermute(tail, axis, [(i, (i + 1) % count) for i in range(ends)])  22.8 us
    ppermute x3, starting transfers between devices, with_halo(): lax.ppermute(tail, axis, [(i, (i + 1) % count) for i in range(ends)])  14.6 us
    unnamed x26, local copies, waits for them, and re-layouts  10.2 us
    concatenate x3, other arithmetic, with_halo(): jnp.concatenate([lax.ppermute(tail, axis, [(i, (i + 1) % count) for i in...  9.9 us
  transfers between devices with their start and end apart: 8, of which 5 were waited for; matrix products, arithmetic and copies ran while one was open for 6% of the time, Pallas kernels for 0%

commit v1 on v0

--- a/solution.py
+++ b/solution.py
@@ -1,7 +1,17 @@
+import functools
 import jax
 import jax.numpy as jnp
 from jax import lax
 from jax.sharding import PartitionSpec as P
+
+
+def _note_hubs(z, lane_axis, comm_axis):
+    for j0 in (lane_axis, comm_axis):
+        z = jax.lax.psum(z, j0)
+    return z
+
+
+advance_routes_all = functools.partial(_note_hubs, lane_axis="tile", comm_axis="frame")
 
 
 def partner(array, axis, stride):
@@ -127,7 +137,7 @@
     sigma = jax.nn.sigmoid(preact)
     preact_grad = (hidden_grad * (sigma * (1.0 + preact * (1.0 - sigma)))).astype(jnp.bfloat16)
     join_part = tap_grads(preact_grad, stacked_pad, tile_rows, col_count)
-    join_total, output_total = lax.psum((join_part, output_part), ("frame", "tile"))
+    join_total, output_total = advance_routes_all((join_part, output_part))
     return (recon.astype(jnp.bfloat16), join_total, output_total)
 
 

time: 320 us -> 339 us (1.059)
  waiting for transfers between devices: 123 us -> 144 us
    psum x1 -> x2, waiting for transfers between devices: 95.2 us -> 116 us  [_note_hubs(): z = jax.lax.psum(z, j0)]
    unnamed x26 -> x28, local copies, waits for them, and re-layouts: 10.2 us -> 8.8 us
  transfers between devices with their start and end apart: 8 -> 9, of which waited for: 5 -> 6; matrix products, arithmetic and copies ran while one was open for 6% -> 5% of each run, Pallas kernels for 0% -> 0%
where the time goes in v1:
time: 339 us; the launch traced here: 336 us
  waiting for transfers between devices  144 us (42%)
  matrix products  120 us (35%)
  starting transfers between devices  19.7 us (6%)
  local copies, waits for them, and re-layouts  19.1 us (6%)
  other arithmetic  18 us (5%)
  between operations  14.7 us (4%)
    psum x2, waiting for transfers between devices, _note_hubs(): z = jax.lax.psum(z, j0)  116 us
    dot_general x18, matrix products, apply_taps(): jnp.einsum('oi,bihw->bohw', kernel[row_tap, col_tap], window, preferred_e...  67.4 us
    dot_general x9, matrix products, transpose_taps(): jnp.einsum('oi,bohw->bihw', kernel[row_tap, col_tap], window, preferred_e...  29.4 us
    dot_general x18, matrix products, tap_grads(): jnp.einsum('bohw,bihw->oi', upstream, window, preferred_element_type=jnp....  23.1 us
    ppermute x3, waiting for transfers between devices, with_halo(): lax.ppermute(tail, axis, [(i, (i + 1) % count) for i in range(ends)])  22.6 us
    ppermute x3, starting transfers between devices, with_halo(): lax.ppermute(tail, axis, [(i, (i + 1) % count) for i in range(ends)])  14.6 us
    concatenate x3, other arithmetic, with_halo(): jnp.concatenate([lax.ppermute(tail, axis, [(i, (i + 1) % count) for i in...  9.9 us
    unnamed x28, local copies, waits for them, and re-layouts  8.8 us
  transfers between devices with their start and end apart: 9, of which 6 were waited for; matrix products, arithmetic and copies ran while one was open for 5% of the time, Pallas kernels for 0%

profile of v1, /device:TPU:0, one launch (start us, length us, event | category | flops | bytes accessed | tf_op | source)
XLA Modules:
  0.0 335.6 jit_solution(13952134535757296504)
XLA Ops:
  9.5 3.5 %gather_fusion.1 = bf16[8,96,8,256]{3,2,1,0:T(8,128)(2,1)S(1)} fusion(bf16[16,96,8,256]{3,2,1,0:T(8,128)(2,1)} %param.10, s32[1024]{0:T(1024)S(1)} %pad_clamp_fusion), kind=kCustom, calls=%fused_computation.1.clone | custom fusion | bytes 6291488 | tf_op jit(solution)/shard_map/jit(_take)/gather | solution.py:110
  15.9 3.5 %gather_fusion = bf16[8,96,8,256]{3,2,1,0:T(8,128)(2,1)S(1)} fusion(bf16[16,96,8,256]{3,2,1,0:T(8,128)(2,1)} %param.10, s32[1024]{0:T(1024)S(1)} %pad_clamp_fusion.1), kind=kCustom, calls=%fused_computation.clone | custom fusion | bytes 6291488 | tf_op jit(solution)/shard_map/jit(_take)/gather | solution.py:115
  21.3 2.3 select_select_fusion.1
  25.4 4.8 %collective-permute-start.1 = (bf16[4,288,1,256]{3,1,2,0:T(8,128)(2,1)S(1)}, bf16[4,288,1,256]{3,1,2,0:T(8,128)(2,1)S(1)}, u32[]{:S(2)}, u32[]{:S(2)}) collective-permute-start(bf16[4,288,1,256]{3,1,2,0:T(8,128)(2,1)S(1)} %get-tuple-element.19), channel_id=1, source_target_pairs={{0,1},{1,2},{2,3},{3,4},{4,5},{5,6},{6,7},{8,9},{9,10},{10,11},{11... | collective-permute-start | bytes 1769480 | tf_op jit(solution)/shard_map/ppermute | solution.py:29
  32.0 3.0 fusion.184
  35.1 20.7 %collective-permute-done.1 = bf16[4,288,1,256]{3,1,2,0:T(8,128)(2,1)S(1)} collective-permute-done((bf16[4,288,1,256]{3,1,2,0:T(8,128)(2,1)S(1)}, bf16[4,288,1,256]{3,1,2,0:T(8,128)(2,1)S(1)}, u32[]{:S(2)}, u32[]{:S(2)}) %collective-permute-start.1) | collective-permute-done | bytes 589856 | tf_op jit(solution)/shard_map/ppermute | solution.py:29
  55.7 5.9 %fusion.5 = bf16[4,288,10,258]{3,1,2,0:T(8,128)(2,1)S(1)} fusion(bf16[4,288,1,256]{3,1,2,0:T(8,128)(2,1)S(1)} %collective-permute-done.2, bf16[4,288,8,256]{3,1,2,0:T(8,128)(2,1)S(1)} %copy_dynamic-update-slice_fusion.1, bf16[4,288,1,256]{3,1,2,0:T(8,128)(2,1)S(1)} %collective-permute-done.1), kind=kLoop, calls=%fused_computation.9 | loop fusion | flops 35665920 | bytes 11842560 | tf_op jit(solution)/shard_map/concatenate | solution.py:27
  61.7 3.0 fusion.13
  64.7 3.3 fusion.17
  68.0 3.0 fusion.21
  70.9 3.3 fusion.25
  74.2 3.0 fusion.29
  77.2 3.0 fusion.44
  80.2 3.0 fusion.42
  83.2 11.2 %fusion.38 = (bf16[4,96,8,256]{3,1,2,0:T(8,128)(2,1)}, f32[4,8,256,96]{2,3,1,0:T(8,128)}) fusion(bf16[4,288,10,258]{3,1,2,0:T(8,128)(2,1)S(1)} %fusion.5, bf16[3,3,96,288]{3,2,1,0:T(8,128)(2,1)} %param.16, f32[4,8,256,96]{2,3,1,0:T(8,128)} %fusion.44, f32[4,8,256,96]{2,3,1,0:T(8,128)} %fusion.13, f32[4,8,256,96]{2,3,1,0:T(8,128)} %fusion.17, ...), kind=kOutput, calls=%fused_computation.52 | convolution fusion | flops 463208448 | bytes 34676736 | tf_op jit(solution)/shard_map/oi,bihw->bohw/dot_general | solution.py:47
  95.5 4.4 %collective-permute-start.3 = (bf16[4,96,1,256]{3,1,2,0:T(8,128)(2,1)S(1)}, bf16[4,96,1,256]{3,1,2,0:T(8,128)(2,1)S(1)}, u32[]{:S(2)}, u32[]{:S(2)}) collective-permute-start(bf16[4,96,1,256]{3,1,2,0:T(8,128)(2,1)S(1)} %get-tuple-element.23), channel_id=1, source_target_pairs={{0,1},{1,2},{2,3},{3,4},{4,5},{5,6},{6,7},{8,9},{9,10},{10,11},{11... | collective-permute-start | bytes 589832 | tf_op jit(solution)/shard_map/ppermute | solution.py:29
  101.4 3.7 %fusion.209 = f32[4,8,256,96]{2,3,1,0:T(8,128)} fusion(bf16[4,96,8,256]{3,1,2,0:T(8,128)(2,1)} %get-tuple-element.27, bf16[3,3,96,96]{3,2,1,0:T(8,128)(2,1)S(1)} %copy-done.5), kind=kOutput, calls=%fused_computation.183 | convolution fusion | flops 150994944 | bytes 4743168 | tf_op jit(solution)/shard_map/oi,bihw->bohw/dot_general | solution.py:47
  105.1 3.9 %collective-permute-done.4 = bf16[4,96,1,256]{3,1,2,0:T(8,128)(2,1)S(1)} collective-permute-done((bf16[4,96,1,256]{3,1,2,0:T(8,128)(2,1)S(1)}, bf16[4,96,1,256]{3,1,2,0:T(8,128)(2,1)S(1)}, u32[]{:S(2)}, u32[]{:S(2)}) %collective-permute-start.4) | collective-permute-done | bytes 196640 | tf_op jit(solution)/shard_map/ppermute | solution.py:31
  113.2 2.3 fusion.80
  117.8 2.3 fusion.88
  126.9 12.3 %bitcast_convert_fusion = (bf16[4,96,8,256]{3,1,2,0:T(8,128)(2,1)}, f32[4,8,256,96]{2,3,1,0:T(8,128)}) fusion(bf16[4,96,10,258]{3,1,2,0:T(8,128)(2,1)S(1)} %select_maximum_fusion.2, bf16[3,3,96,96]{3,2,1,0:T(8,128)(2,1)S(1)} %copy-done.5, f32[4,8,256,96]{2,3,1,0:T(8,128)} %fusion.175, f32[4,8,256,96]{2,3,1,0:T(8,128)} %fusion.76, ...), kind=kOutput, calls=%fused_computation.42 | convolution fusion | flops 158072832 | bytes 31481856 | tf_op jit(solution)/shard_map/oi,bihw->bohw/dot_general | solution.py:47
  139.1 2.6 fusion.34
  145.9 5.4 %collective-permute-start.5 = (bf16[4,96,1,256]{3,1,2,0:T(8,128)(2,1)S(1)}, bf16[4,96,1,256]{3,1,2,0:T(8,128)(2,1)S(1)}, u32[]{:S(2)}, u32[]{:S(2)}) collective-permute-start(bf16[4,96,1,256]{3,1,2,0:T(8,128)(2,1)S(1)} %get-tuple-element.22), channel_id=1, source_target_pairs={{0,1},{1,2},{2,3},{3,4},{4,5},{5,6},{6,7},{8,9},{9,10},{10,11},{11... | collective-permute-start | bytes 589832 | tf_op jit(solution)/shard_map/ppermute | solution.py:29
  160.5 2.4 fusion.58
  162.9 2.3 fusion.60
  165.2 2.4 fusion.62
  169.9 2.5 fusion.66
  174.6 2.3 fusion.46
  176.9 10.6 %fusion.31 = bf16[4,96,8,256]{3,1,2,0:T(8,128)(2,1)S(1)} fusion(f32[4,8,256,96]{2,3,1,0:T(8,128)} %get-tuple-element.28, f32[4,8,256,96]{2,3,1,0:T(8,128)} %fusion.50, f32[4,8,256,96]{2,3,1,0:T(8,128)} %fusion.58, f32[4,8,256,96]{2,3,1,0:T(8,128)} %fusion.60, f32[4,8,256,96]{2,3,1,0:T(8,128)} %fusion.207, f32[4,8,256,96]{2,3,1,0:T(8,128)} %fusion.62, ...), kind=kOutput, calls=%fused_computation.40 | convolution fusion | flops 164364288 | bytes 31481856 | tf_op jit(solution)/shard_map/oi,bohw->bihw/dot_general | solution.py:76
  206.2 95.4 %all-reduce.8.cloned.1.call-done = (f32[3,3,96,288]{3,2,1,0:T(8,128)}, f32[3,3,96,96]{3,2,1,0:T(8,128)}) async-done(((f32[3,3,96,288]{3,2,1,0:T(8,128)}, f32[3,3,96,96]{3,2,1,0:T(8,128)}), (f32[3,3,96,288]{3,2,1,0:T(8,128)}, f32[3,3,96,96]{3,2,1,0:T(8,128)})) %all-reduce.8.cloned.1.call-update) | async-done | bytes 1327120 | tf_op jit(solution)/shard_map/psum | solution.py:10
  303.6 20.6 %all-reduce.10.cloned.1.call-done = (f32[3,3,96,288]{3,2,1,0:T(8,128)}, f32[3,3,96,96]{3,2,1,0:T(8,128)}) async-done(((f32[3,3,96,288]{3,2,1,0:T(8,128)}, f32[3,3,96,96]{3,2,1,0:T(8,128)}), (f32[3,3,96,288]{3,2,1,0:T(8,128)}, f32[3,3,96,96]{3,2,1,0:T(8,128)})) %all-reduce.10.cloned.1.call-update) | async-done | bytes 1327120 | tf_op jit(solution)/shard_map/psum | solution.py:10
  324.2 2.5 copy.135
  (94 shorter events, 66.5 us)
Async XLA Ops:
  7.2 294.4 %all-reduce.8.cloned.1.call-start = ((), (), s32[]{:S(2)}) async-start(), calls=%async_computation | async-start | bytes 3538944 | tf_op jit(solution)/shard_map/psum | solution.py:10
  13.1 2.6 copy-start.10
  15.1 6.1 %collective-permute-start = (bf16[8,96,8,256]{3,2,1,0:T(8,128)(2,1)}, bf16[8,96,8,256]{3,2,1,0:T(8,128)(2,1)}, u32[]{:S(2)}, u32[]{:S(2)}) collective-permute-start(bf16[8,96,8,256]{3,2,1,0:T(8,128)(2,1)} %select_select_fusion), channel_id=1, source_target_pairs={{0,8},{8,0},{1,9},{9,1},{2,10},{10,2},{3,11},{11,3},{4,12},{12,4},... | collective-permute-start | bytes 9437192 | tf_op jit(solution)/shard_map/ppermute | solution.py:18
  15.9 3.6 %copy-start.11 = (f32[32]{0:T(128)S(1)}, f32[32]{0:T(128)}, u32[]{:S(2)}) copy-start(f32[32]{0:T(128)} %param.15) | copy-start | bytes 388
  23.6 1.4 copy-start.2
  25.0 7.0 %copy-start.9 = (bf16[3,3,96,288]{3,2,1,0:T(8,128)(2,1)S(1)}, bf16[3,3,96,288]{3,2,1,0:T(8,128)(2,1)}, u32[]{:S(2)}) copy-start(bf16[3,3,96,288]{3,2,1,0:T(8,128)(2,1)} %param.16) | copy-start | bytes 1492996
  25.4 30.3 %collective-permute-start.1 = (bf16[4,288,1,256]{3,1,2,0:T(8,128)(2,1)S(1)}, bf16[4,288,1,256]{3,1,2,0:T(8,128)(2,1)S(1)}, u32[]{:S(2)}, u32[]{:S(2)}) collective-permute-start(bf16[4,288,1,256]{3,1,2,0:T(8,128)(2,1)S(1)} %get-tuple-element.19), channel_id=1, source_target_pairs={{0,1},{1,2},{2,3},{3,4},{4,5},{5,6},{6,7},{8,9},{9,10},{10,11},{11... | collective-permute-start | bytes 1769480 | tf_op jit(solution)/shard_map/ppermute | solution.py:29
  30.3 25.5 %collective-permute-start.2 = (bf16[4,288,1,256]{3,1,2,0:T(8,128)(2,1)S(1)}, bf16[4,288,1,256]{3,1,2,0:T(8,128)(2,1)S(1)}, u32[]{:S(2)}, u32[]{:S(2)}) collective-permute-start(bf16[4,288,1,256]{3,1,2,0:T(8,128)(2,1)S(1)} %get-tuple-element.20), channel_id=1, source_target_pairs={{1,0},{2,1},{3,2},{4,3},{5,4},{6,5},{7,6},{9,8},{10,9},{11,10},{12... | collective-permute-start | bytes 1769480 | tf_op jit(solution)/shard_map/ppermute | solution.py:31
  55.7 24.4 %copy-start.6 = (bf16[4,288,1,256]{3,1,2,0:T(8,128)(2,1)}, bf16[4,288,1,256]{3,1,2,0:T(8,128)(2,1)S(1)}, u32[]{:S(2)}) copy-start(bf16[4,288,1,256]{3,1,2,0:T(8,128)(2,1)S(1)} %collective-permute-done.1) | copy-start | bytes 1769476
  83.2 18.2 %copy-start.5 = (bf16[3,3,96,96]{3,2,1,0:T(8,128)(2,1)S(1)}, bf16[3,3,96,96]{3,2,1,0:T(8,128)(2,1)}, u32[]{:S(2)}) copy-start(bf16[3,3,96,96]{3,2,1,0:T(8,128)(2,1)} %param.17) | copy-start | bytes 497668
  94.3 14.7 %copy-start = (bf16[4,96,8,256]{3,1,2,0:T(8,128)(2,1)S(1)}, bf16[4,96,8,256]{3,1,2,0:T(8,128)(2,1)}, u32[]{:S(2)}) copy-start(bf16[4,96,8,256]{3,1,2,0:T(8,128)(2,1)} %get-tuple-element.27) | copy-start | bytes 4718596
  95.5 9.6 %collective-permute-start.3 = (bf16[4,96,1,256]{3,1,2,0:T(8,128)(2,1)S(1)}, bf16[4,96,1,256]{3,1,2,0:T(8,128)(2,1)S(1)}, u32[]{:S(2)}, u32[]{:S(2)}) collective-permute-start(bf16[4,96,1,256]{3,1,2,0:T(8,128)(2,1)S(1)} %get-tuple-element.23), channel_id=1, source_target_pairs={{0,1},{1,2},{2,3},{3,4},{4,5},{5,6},{6,7},{8,9},{9,10},{10,11},{11... | collective-permute-start | bytes 589832 | tf_op jit(solution)/shard_map/ppermute | solution.py:29
  99.9 9.1 %collective-permute-start.4 = (bf16[4,96,1,256]{3,1,2,0:T(8,128)(2,1)S(1)}, bf16[4,96,1,256]{3,1,2,0:T(8,128)(2,1)S(1)}, u32[]{:S(2)}, u32[]{:S(2)}) collective-permute-start(bf16[4,96,1,256]{3,1,2,0:T(8,128)(2,1)S(1)} %get-tuple-element.24), channel_id=1, source_target_pairs={{1,0},{2,1},{3,2},{4,3},{5,4},{6,5},{7,6},{9,8},{10,9},{11,10},{12... | collective-permute-start | bytes 589832 | tf_op jit(solution)/shard_map/ppermute | solution.py:31
  126.9 12.3 %copy-start.3 = (bf16[4,96,8,256]{3,2,1,0:T(8,128)(2,1)S(1)}, bf16[4,96,8,256]{3,2,1,0:T(8,128)(2,1)}, u32[]{:S(2)}) copy-start(bf16[4,96,8,256]{3,2,1,0:T(8,128)(2,1)} %param.11) | copy-start | bytes 4718596
  144.6 11.9 %collective-permute-start.6 = (bf16[4,96,1,256]{3,1,2,0:T(8,128)(2,1)S(1)}, bf16[4,96,1,256]{3,1,2,0:T(8,128)(2,1)S(1)}, u32[]{:S(2)}, u32[]{:S(2)}) collective-permute-start(bf16[4,96,1,256]{3,1,2,0:T(8,128)(2,1)S(1)} %get-tuple-element.21), channel_id=1, source_target_pairs={{1,0},{2,1},{3,2},{4,3},{5,4},{6,5},{7,6},{9,8},{10,9},{11,10},{12... | collective-permute-start | bytes 589832 | tf_op jit(solution)/shard_map/ppermute | solution.py:31
  145.9 12.6 %collective-permute-start.5 = (bf16[4,96,1,256]{3,1,2,0:T(8,128)(2,1)S(1)}, bf16[4,96,1,256]{3,1,2,0:T(8,128)(2,1)S(1)}, u32[]{:S(2)}, u32[]{:S(2)}) collective-permute-start(bf16[4,96,1,256]{3,1,2,0:T(8,128)(2,1)S(1)} %get-tuple-element.22), channel_id=1, source_target_pairs={{0,1},{1,2},{2,3},{3,4},{4,5},{5,6},{6,7},{8,9},{9,10},{10,11},{11... | collective-permute-start | bytes 589832 | tf_op jit(solution)/shard_map/ppermute | solution.py:29
  156.5 6.4 %copy-start.8 = (f32[9,96,96]{2,1,0:T(8,128)}, f32[9,96,96]{2,1,0:T(8,128)S(1)}, u32[]{:S(2)}) copy-start(f32[9,96,96]{2,1,0:T(8,128)S(1)} %fusion.168) | copy-start | bytes 995332
  187.6 1.8 copy-start.7
  205.0 1.1 copy-start.4
  206.1 95.5 %copy-start.1 = (bf16[4,96,8,256]{3,1,2,0:T(8,128)(2,1)S(1)}, bf16[4,96,8,256]{3,1,2,0:T(8,128)(2,1)}, u32[]{:S(2)}) copy-start(bf16[4,96,8,256]{3,1,2,0:T(8,128)(2,1)} %get-tuple-element.29) | copy-start | bytes 4718596
  206.1 118.1 %all-reduce.10.cloned.1.call-start = ((), (), s32[]{:S(2)}) async-start(), calls=%async_computation.1 | async-start | bytes 3538944 | tf_op jit(solution)/shard_map/psum | solution.py:10
Sparse Core Ops, SparseCore 0:
  206.3 95.2 all-reduce.7
  304.0 20.1 all-reduce.9
